TPU v7x, 512 devices: a whole 4x8x8 slice. The times are simulated.
512 devices in a mesh: bank: 32 (over y, x), zero: 16 (over z, core).
Axes of the slice: x: 4, y: 8, z: 8, core: 2. Of those that a mesh axis runs over, the one named last changes fastest.
Arguments:
- master_down: float32 [64, 1024, 2048], P('bank', None, 'zero'), may hold values from -0.25 to 0.25
- router_weight: float32 [2048, 64], P('zero', 'bank'), may hold values from -0.125 to 0.125
- router_gain: float32 [2048], P('zero'), may hold values from 0.25 to 1.75
Outputs:
- final_down: bfloat16 [64, 1024, 2048], P('bank')
- scale_down: float32 [64, 1024], P('bank')
- serve_router: bfloat16 [2048, 64], replicated
All inputs are finite; a program needn't handle non-finite values. Where the computation divides by a largest or mean magnitude, that divisor is 1e-20 or more.
Results may differ from a plain program's by a relative error of at most 0.001.
Values may be sent and summed in bfloat16 or wider, within the bound.
A program may use at most 64 MiB of HBM per device.

v0:
```python
import jax
import jax.numpy as jnp
from jax import lax
from jax.sharding import PartitionSpec as P


def copy_for_each(array, axis):
    count = lax.axis_size(axis)
    return lax.all_to_all(
        jnp.broadcast_to(array[None], (count, *array.shape)), axis, 0, 0, tiled=True
    )


def of_everyone(array, axis):
    return copy_for_each(array, axis).max(axis=0)


def joined_along(pieces, dim):
    pieces = jnp.moveaxis(pieces, 0, dim)
    shape = pieces.shape
    return pieces.reshape(*shape[:dim], shape[dim] * shape[dim + 1], *shape[dim + 2 :])


def collect(array, axis, dim):
    return joined_along(copy_for_each(array, axis), dim)


def per_device(master_down, router_weight, router_gain):
    scale_down = of_everyone(jnp.max(jnp.abs(master_down), axis=2), "zero")
    narrow_down = (master_down / jnp.expand_dims(scale_down, 2)).astype(jnp.bfloat16)
    final_down = lax.all_gather(narrow_down, "zero", axis=2, tiled=True)
    part_router = (router_weight * router_gain[:, None]).astype(jnp.bfloat16)
    row_router = lax.all_gather(part_router, "zero", axis=0, tiled=True)
    serve_router = collect(row_router, "bank", 1)
    return (final_down, scale_down, serve_router)


def solution(mesh):
    placed = (P("bank", None, "zero"), P("zero", "bank"), P("zero"))
    return jax.shard_map(
        per_device,
        mesh=mesh,
        in_specs=placed,
        out_specs=(P("bank", None, None), P("bank", None), P()),
        check_vma=False,
    )
```

profile of v0, /device:TPU:1, one launch (start us, length us, event | category | flops | bytes accessed | tf_op | source)
XLA Modules:
  0.0 114.2 jit_solution(8607611359955756124)
XLA Ops:
  7.2 0.0 all-gather.2.cloned.1.call-start
  7.2 1.6 %abs_reduce_fusion = f32[2,1024]{1,0:T(2,128)S(1)} fusion(f32[2,1024,128]{2,1,0:T(8,128)} %param.3), kind=kLoop, calls=%fused_computation.1 | loop fusion | flops 522240 | bytes 1056768 | tf_op jit(solution)/shard_map/reduce_max | solution.py:29
  8.8 20.5 %all_to_all.10 = f32[16,2,1024]{2,1,0:T(2,128)S(1)} all-to-all(f32[16,2,1024]{2,1,0:T(2,128)S(1)} %broadcast_in_dim.4), channel_id=1, replica_groups=mesh['bank'=32,'zero'=16] {'zero'}, dimensions={0} | all-to-all | bytes 262144 | tf_op jit(solution)/shard_map/all_to_all | solution.py:9
  29.3 0.1 reduce_max.19
  29.4 0.0 copy-start
  29.4 2.4 %divide_convert_fusion = bf16[2,1024,128]{2,1,0:T(8,128)(2,1)} fusion(f32[2,1024,128]{2,1,0:T(8,128)} %param.3, f32[2,1024]{1,0:T(2,128)S(1)} %reduce_max.19), kind=kLoop, calls=%fused_computation | loop fusion | flops 524288 | bytes 1581056 | tf_op jit(solution)/shard_map/convert_element_type | solution.py:30
  31.8 0.0 all-gather.2.cloned.1.call-update
  31.8 0.7 multiply_convert_fusion
  32.5 14.5 %all_gather.7 = bf16[2048,2]{0,1:T(2,128)(2,1)S(1)} all-gather(bf16[128,2]{0,1:T(2,128)(2,1)S(1)} %multiply_convert_fusion), channel_id=1, replica_groups=mesh['bank'=32,'zero'=16] {'zero'}, dimensions={0}, use_global_device_ids=true | all-gather | bytes 8704 | tf_op jit(solution)/shard_map/all_gather | solution.py:33
  46.9 0.1 broadcast_in_dim.5
  47.1 21.1 %all_to_all.11 = bf16[32,2048,2]{1,2,0:T(2,128)(2,1)S(1)} all-to-all(bf16[32,2048,2]{1,2,0:T(2,128)(2,1)S(1)} %broadcast_in_dim.5), channel_id=1, replica_groups=mesh['bank'=32,'zero'=16] {'bank'}, dimensions={0} | all-to-all | bytes 524288 | tf_op jit(solution)/shard_map/all_to_all | solution.py:9
  68.2 0.8 reshape.13
  69.0 29.9 %all-gather.2.cloned.1.call-done = bf16[2,1024,2048]{2,1,0:T(8,128)(2,1)} async-done(((bf16[2,1024,128]{2,1,0:T(8,128)(2,1)}), bf16[2,1024,2048]{2,1,0:T(8,128)(2,1)}) %all-gather.2.cloned.1.call-update) | async-done | bytes 8388624 | tf_op jit(solution)/shard_map/all_gather | solution.py:31
  98.9 8.4 %copy.9 = bf16[2,1024,2048]{2,1,0:T(8,128)(2,1)} copy(bf16[2,1024,2048]{2,1,0:T(8,128)(2,1)} %all-gather.2.cloned.1.call-done) | data formatting | bytes 16777216
  107.3 0.0 copy-done
  (1 shorter events, 0.0 us)
Async XLA Ops:
  7.2 91.7 %all-gather.2.cloned.1.call-start = ((), (), s32[]{:S(2)}) async-start(), calls=%async_computation.2 | async-start | bytes 8912896 | tf_op jit(solution)/shard_map/all_gather | solution.py:31
  29.4 77.9 %copy-start = (f32[2,1024]{1,0:T(2,128)}, f32[2,1024]{1,0:T(2,128)S(1)}, u32[]{:S(2)}) copy-start(f32[2,1024]{1,0:T(2,128)S(1)} %reduce_max.19) | copy-start | bytes 24580
Sparse Core Ops, SparseCore 0:
  31.9 66.9 all-gather.1
where the time goes:
time: 114 us
  blocking collectives  56.1 us (49%)
  waiting for transfers between devices  29.9 us (26%)
  between operations  14.1 us (12%)
  local copies, waits for them, and re-layouts  9.42 us (8%)
  other arithmetic  4.68 us (4%)
    all_to_all x2, blocking collectives, copy_for_each(): lax.all_to_all(jnp.broadcast_to(array[None], (count, *array.shape)), axis...  41.6 us
    all_gather x1, waiting for transfers between devices, per_device(): final_down = lax.all_gather(narrow_down, 'zero', axis=2, tiled=True)  29.9 us
    all_gather x1, blocking collectives, per_device(): row_router = lax.all_gather(part_router, 'zero', axis=0, tiled=True)  14.5 us
    unnamed x3, local copies, waits for them, and re-layouts  8.44 us
    convert_element_type x1, other arithmetic, per_device(): (master_down / jnp.expand_dims(scale_down, 2)).astype(jnp.bfloat16)  2.36 us
  transfers between devices with their start and end apart: 1, of which 1 were waited for; matrix products, arithmetic and copies ran while one was open for 1% of the time, Pallas kernels for 0%

commit v1 on v0

--- a/solution.py
+++ b/solution.py
@@ -28,7 +28,9 @@
 def per_device(master_down, router_weight, router_gain):
     scale_down = of_everyone(jnp.max(jnp.abs(master_down), axis=2), "zero")
     narrow_down = (master_down / jnp.expand_dims(scale_down, 2)).astype(jnp.bfloat16)
-    final_down = lax.all_gather(narrow_down, "zero", axis=2, tiled=True)
+    final_down = jnp.concatenate(
+        lax.all_to_all(jnp.stack([narrow_down] * lax.axis_size("zero")), "zero", 0, 0), axis=2
+    )
     part_router = (router_weight * router_gain[:, None]).astype(jnp.bfloat16)
     row_router = lax.all_gather(part_router, "zero", axis=0, tiled=True)
     serve_router = collect(row_router, "bank", 1)

time: 114 us -> 275 us (2.41)
  waiting for transfers between devices: 29.9 us -> 193 us
  blocking collectives: 56.1 us -> 17.2 us
  starting transfers between devices: 0.04 us -> 28.9 us
  local copies, waits for them, and re-layouts: 9.42 us -> 31.1 us
  between operations: 14.1 us -> 0.67 us
    all_to_all x0 -> x3, waiting for transfers between devices: none -> 193 us  [the longest x1 183 us: per_device(): lax.all_to_all(jnp.stack([narrow_down] * lax.axis_size('zero')), 'zero',...]
    all_to_all x2 -> x0, blocking collectives: 41.6 us -> none  [copy_for_each(): lax.all_to_all(jnp.broadcast_to(array[None], (count, *array.shape)), axis...]
    all_gather x1 -> x0, waiting for transfers between devices: 29.9 us -> none  [per_device(): final_down = lax.all_gather(narrow_down, 'zero', axis=2, tiled=True)]
    all_to_all x0 -> x3, starting transfers between devices: none -> 28.9 us  [the longest x2 21.5 us: copy_for_each(): lax.all_to_all(jnp.broadcast_to(array[None], (count, *array.shape)), axis...]
    all_to_all x0 -> x1, local copies, waits for them, and re-layouts: none -> 11.9 us  [per_device(): lax.all_to_all(jnp.stack([narrow_down] * lax.axis_size('zero')), 'zero',...]
    another operation x0 -> x1, local copies, waits for them, and re-layouts: none -> 5.28 us  [per_device(): jnp.stack([narrow_down] * lax.axis_size('zero'))]
    unnamed x3, local copies, waits for them, and re-layouts: 8.44 us -> 11.6 us
  transfers between devices with their start and end apart: 1 -> 3, of which waited for: 1 -> 2; matrix products, arithmetic and copies ran while one was open for 1% -> 1% of each run, Pallas kernels for 0% -> 0%
where the time goes in v1:
time: 275 us; the launch traced here: 274 us
  waiting for transfers between devices  193 us (70%)
  local copies, waits for them, and re-layouts  31.1 us (11%)
  starting transfers between devices  28.9 us (11%)
  blocking collectives  17.2 us (6%)
  other arithmetic  3.88 us (1%)
    all_to_all x1, waiting for transfers between devices, per_device(): lax.all_to_all(jnp.stack([narrow_down] * lax.axis_size('zero')), 'zero',...  183 us
    all_to_all x2, starting transfers between devices, copy_for_each(): lax.all_to_all(jnp.broadcast_to(array[None], (count, *array.shape)), axis...  21.5 us
    all_gather x1, blocking collectives, per_device(): row_router = lax.all_gather(part_router, 'zero', axis=0, tiled=True)  17.2 us
    all_to_all x1, local copies, waits for them, and re-layouts, per_device(): lax.all_to_all(jnp.stack([narrow_down] * lax.axis_size('zero')), 'zero',...  11.9 us
    unnamed x3, local copies, waits for them, and re-layouts  11.6 us
    all_to_all x2, waiting for transfers between devices, copy_for_each(): lax.all_to_all(jnp.broadcast_to(array[None], (count, *array.shape)), axis...  10 us
    all_to_all x1, starting transfers between devices, per_device(): lax.all_to_all(jnp.stack([narrow_down] * lax.axis_size('zero')), 'zero',...  7.46 us
  transfers between devices with their start and end apart: 3, of which 2 were waited for; matrix products, arithmetic and copies ran while one was open for 1% of the time, Pallas kernels for 0%

profile of v1, /device:TPU:1, one launch (start us, length us, event | category | flops | bytes accessed | tf_op | source)
XLA Modules:
  0.0 274.4 jit_solution(10368530397778361359)
XLA Ops:
  0.6 1.6 abs_reduce_fusion
  2.2 0.7 broadcast_in_dim.4
  2.9 11.8 %all-to-all-start = ((f32[16,2,1024]{2,1,0:T(2,128)}), f32[16,2,1024]{2,1,0:T(2,128)S(1)}, u32[]{:S(2)}, u32[]{:S(2)}) async-start(f32[16,2,1024]{2,1,0:T(2,128)} %broadcast_in_dim.4), calls=%async_computation | async-start | bytes 262144 | tf_op jit(solution)/shard_map/all_to_all | solution.py:9
  14.7 0.7 multiply_convert_fusion
  15.4 17.2 %all_gather.3 = bf16[2048,2]{0,1:T(2,128)(2,1)S(1)} all-gather(bf16[128,2]{0,1:T(2,128)(2,1)S(1)} %multiply_convert_fusion), channel_id=1, replica_groups=mesh['bank'=32,'zero'=16] {'zero'}, dimensions={0}, use_global_device_ids=true | all-gather | bytes 8704 | tf_op jit(solution)/shard_map/all_gather | solution.py:35
  32.6 0.0 all-to-all-done
  32.6 0.8 broadcast_in_dim.5
  33.4 9.7 %all-to-all-start.2 = ((bf16[32,2048,2]{1,2,0:T(2,128)(2,1)}), bf16[32,2048,2]{1,2,0:T(2,128)(2,1)S(1)}, u32[]{:S(2)}, u32[]{:S(2)}) async-start(bf16[32,2048,2]{1,2,0:T(2,128)(2,1)} %broadcast_in_dim.5), calls=%async_computation.2 | async-start | bytes 524288 | tf_op jit(solution)/shard_map/all_to_all | solution.py:9
  43.1 0.1 reduce_max.19
  43.2 0.0 copy-start
  43.2 1.6 divide_convert_fusion
  44.8 10.0 %all-to-all-done.2 = bf16[32,2048,2]{1,2,0:T(2,128)(2,1)S(1)} async-done(((bf16[32,2048,2]{1,2,0:T(2,128)(2,1)}), bf16[32,2048,2]{1,2,0:T(2,128)(2,1)S(1)}, u32[]{:S(2)}, u32[]{:S(2)}) %all-to-all-start.2) | async-done | bytes 262176 | tf_op jit(solution)/shard_map/all_to_all | solution.py:9
  54.8 5.3 %stack.2 = bf16[16,2,1024,128]{3,2,1,0:T(8,128)(2,1)} broadcast(bf16[2,1024,128]{2,1,0:T(8,128)(2,1)S(1)} %divide_convert_fusion), dimensions={1,2,3} | broadcast | bytes 8912896 | tf_op jit(solution)/shard_map/stack | solution.py:32
  60.0 0.0 copy-done
  60.0 7.5 %all-to-all-start.1 = ((bf16[16,2,1024,128]{3,2,1,0:T(8,128)(2,1)}), bf16[16,2,1024,128]{3,2,1,0:T(8,128)(2,1)}, u32[]{:S(2)}, u32[]{:S(2)}) async-start(bf16[16,2,1024,128]{3,2,1,0:T(8,128)(2,1)} %stack.2), calls=%async_computation.1 | async-start | bytes 16777216 | tf_op jit(solution)/shard_map/all_to_all | solution.py:32
  67.5 0.8 reshape.23
  68.3 182.6 %all-to-all-done.1 = bf16[16,2,1024,128]{3,2,1,0:T(8,128)(2,1)} async-done(((bf16[16,2,1024,128]{3,2,1,0:T(8,128)(2,1)}), bf16[16,2,1024,128]{3,2,1,0:T(8,128)(2,1)}, u32[]{:S(2)}, u32[]{:S(2)}) %all-to-all-start.1) | async-done | bytes 8388640 | tf_op jit(solution)/shard_map/all_to_all | solution.py:32
  250.9 11.9 %copy.11 = bf16[16,2,1024,128]{2,3,0,1:T(8,128)(2,1)} copy(bf16[16,2,1024,128]{3,2,1,0:T(8,128)(2,1)} %all-to-all-done.1) | data formatting | bytes 16777216 | tf_op jit(solution)/shard_map/all_to_all | solution.py:32
  262.8 11.6 %copy.12 = bf16[2,1024,2048]{2,1,0:T(8,128)(2,1)} copy(bf16[2,1024,2048]{1,2,0:T(8,128)(2,1)} %bitcast.6) | data formatting | bytes 16777216
Async XLA Ops:
  2.9 29.7 %all-to-all-start = ((f32[16,2,1024]{2,1,0:T(2,128)}), f32[16,2,1024]{2,1,0:T(2,128)S(1)}, u32[]{:S(2)}, u32[]{:S(2)}) async-start(f32[16,2,1024]{2,1,0:T(2,128)} %broadcast_in_dim.4), calls=%async_computation | async-start | bytes 262144 | tf_op jit(solution)/shard_map/all_to_all | solution.py:9
  33.4 21.3 %all-to-all-start.2 = ((bf16[32,2048,2]{1,2,0:T(2,128)(2,1)}), bf16[32,2048,2]{1,2,0:T(2,128)(2,1)S(1)}, u32[]{:S(2)}, u32[]{:S(2)}) async-start(bf16[32,2048,2]{1,2,0:T(2,128)(2,1)} %broadcast_in_dim.5), calls=%async_computation.2 | async-start | bytes 524288 | tf_op jit(solution)/shard_map/all_to_all | solution.py:9
  43.2 16.9 %copy-start = (f32[2,1024]{1,0:T(2,128)}, f32[2,1024]{1,0:T(2,128)S(1)}, u32[]{:S(2)}) copy-start(f32[2,1024]{1,0:T(2,128)S(1)} %reduce_max.19) | copy-start | bytes 24580
  60.0 190.8 %all-to-all-start.1 = ((bf16[16,2,1024,128]{3,2,1,0:T(8,128)(2,1)}), bf16[16,2,1024,128]{3,2,1,0:T(8,128)(2,1)}, u32[]{:S(2)}, u32[]{:S(2)}) async-start(bf16[16,2,1024,128]{3,2,1,0:T(8,128)(2,1)} %stack.2), calls=%async_computation.1 | async-start | bytes 16777216 | tf_op jit(solution)/shard_map/all_to_all | solution.py:32
